TPU v7x, 256 devices: a whole 4x4x8 slice. The times are simulated.
256 devices in a mesh: dp: 8 (over z_hi, x), tensor: 8 (over z_lo, core), fsdp: 4 (over y).
Axes of the slice: x: 4, y: 4, z: 8 (z_hi: 2, z_lo: 4; z = z_hi * 4 + z_lo), core: 2. Of those that a mesh axis runs over, the one named last changes fastest.
Arguments:
- train_acts: bfloat16 [8192, 4096], P(('dp', 'fsdp'), 'tensor'), may hold values from -6 to 6
- val_acts: bfloat16 [8192, 4096], P(('dp', 'fsdp'), 'tensor'), may hold values from -6 to 6
- train_cot: bfloat16 [8192, 4096], P(('dp', 'fsdp'), 'tensor'), may hold values from -6 to 6
- val_cot: bfloat16 [8192, 4096], P(('dp', 'fsdp'), 'tensor'), may hold values from -6 to 6
- train_lengths: int32 [128], P(('dp', 'fsdp')), may hold values from 16 to 64
- val_lengths: int32 [128], P(('dp', 'fsdp')), may hold values from 16 to 64
- gate_weight: bfloat16 [4096, 11008], P(('dp', 'fsdp'), 'tensor'), may hold values from -0.09375 to 0.09375
- up_weight: bfloat16 [4096, 11008], P(('dp', 'fsdp'), 'tensor'), may hold values from -0.09375 to 0.09375
- in_basis: bfloat16 [11008, 64], P('tensor'), may hold values from -0.0546875 to 0.0546875
- out_basis: bfloat16 [4096, 128], P('tensor'), may hold values from -0.09375 to 0.09375
Outputs:
- scores: float32 [128, 128], P(('dp', 'fsdp'))
Inputs may be any that keep to these rules, and one draw needn't show every extreme that they name: `train_lengths`: an example's first length slots hold its tokens, the rest are padding. `val_lengths`: as for the training examples.
All inputs are finite; a program needn't handle non-finite values.
Results may differ from a plain program's by a relative error of at most 0.004.
Values may be sent and summed in bfloat16 or wider, within the bound.
A program may use at most 128 MiB of HBM per device.

v0:
```python
import jax
import jax.numpy as jnp
from jax import lax
from jax.sharding import PartitionSpec as P

SEQ = 64


def side_by_side(arrays, axis, dim, along):
    widths = [a.shape[along] for a in arrays]
    both = jnp.concatenate(arrays, axis=along)
    out = lax.all_gather(both, axis, axis=dim, tiled=True)
    return tuple(jnp.split(out, [sum(widths[:k]) for k in range(1, len(widths))], axis=along))


def from_everyone(array, axis):
    copies = jnp.broadcast_to(array, (lax.axis_size(axis), *array.shape))
    return lax.all_to_all(copies, axis, split_axis=0, concat_axis=0, tiled=True)


def taken_together(array, axis):
    return from_everyone(array, axis).sum(axis=0)


def in_blocks(array, dim, count):
    shape = array.shape
    tiles = array.reshape(*shape[:dim], count, shape[dim] // count, *shape[dim + 1 :])
    return jnp.moveaxis(tiles, dim, 0)


def summed_on_arrival(array, axis, dim):
    tiles = in_blocks(array, dim, lax.axis_size(axis))
    arrived = lax.all_to_all(tiles, axis, split_axis=0, concat_axis=0, tiled=True)
    return arrived.sum(axis=0)


def laid_out(tiles, dim):
    shape = list(tiles.shape[1:])
    shape[dim] *= tiles.shape[0]
    return jnp.moveaxis(tiles, 0, dim).reshape(shape)


def gather_directly(array, axis, dim):
    tiles = from_everyone(array, axis)
    return laid_out(tiles, dim)


def outer_sums(in_proj, out_proj, valid):
    in_three = in_proj.reshape(valid.shape[0], valid.shape[1], in_proj.shape[1]) * valid[:, :, None]
    out_three = out_proj.reshape(valid.shape[0], valid.shape[1], out_proj.shape[1])
    return jnp.einsum("esj,esk->ejk", in_three, out_three, precision=lax.Precision.HIGHEST)


def on_device(
    train_acts,
    val_acts,
    train_cot,
    val_cot,
    train_lengths,
    val_lengths,
    gate_weight,
    up_weight,
    in_basis,
    out_basis,
):
    train_full, val_full = side_by_side((train_acts, val_acts), "tensor", 1, 0)
    activations = jnp.concatenate([train_full, val_full], axis=0)
    cotangents = jnp.concatenate([train_cot, val_cot], axis=0)
    pieces = side_by_side((gate_weight, up_weight), ("dp", "fsdp"), 0, 1)
    gate_sum = jnp.dot(activations, pieces[0], preferred_element_type=jnp.float32)
    up_sum = jnp.dot(activations, pieces[1], preferred_element_type=jnp.float32)
    hidden = (jax.nn.silu(gate_sum) * up_sum).astype(jnp.bfloat16)
    in_part = jnp.dot(hidden, in_basis, preferred_element_type=jnp.float32)
    out_part = jnp.dot(cotangents, out_basis, preferred_element_type=jnp.float32)
    lengths = jnp.concatenate([train_lengths, val_lengths], axis=0)
    valid = (jnp.arange(SEQ, dtype=jnp.int32)[None, :] < lengths[:, None]).astype(jnp.float32)
    out_proj = taken_together(out_part, "tensor")
    partial_value = outer_sums(in_part, out_proj, valid)
    shares = summed_on_arrival(partial_value, "tensor", 1)
    sketch = gather_directly(shares, "tensor", 1)
    flat_sketch = sketch.reshape(sketch.shape[0], sketch.shape[1] * sketch.shape[2])
    unit_rows = flat_sketch * lax.rsqrt(
        jnp.sum(flat_sketch * flat_sketch, axis=1, keepdims=True) + 1e-06
    )
    train_count = train_lengths.shape[0]
    train_unit = unit_rows[:train_count]
    val_local = unit_rows[train_count:]
    width_all = flat_sketch.shape[1]
    share = width_all // lax.axis_size("tensor")
    first = lax.axis_index("tensor") * share
    train_share = lax.dynamic_slice_in_dim(train_unit, first, share, 1)
    val_share_local = lax.dynamic_slice_in_dim(val_local, first, share, 1)
    val_share = gather_directly(val_share_local, ("dp", "fsdp"), 0)
    partial_scores = jnp.dot(
        train_share,
        val_share.T,
        precision=lax.Precision.HIGHEST,
        preferred_element_type=jnp.float32,
    )
    product = lax.psum(partial_scores, "tensor")
    return product * jnp.sqrt(jnp.float32(width_all))


def solution(mesh):
    placed = (
        P(("dp", "fsdp"), "tensor"),
        P(("dp", "fsdp"), "tensor"),
        P(("dp", "fsdp"), "tensor"),
        P(("dp", "fsdp"), "tensor"),
        P(("dp", "fsdp")),
        P(("dp", "fsdp")),
        P(("dp", "fsdp"), "tensor"),
        P(("dp", "fsdp"), "tensor"),
        P("tensor", None),
        P("tensor", None),
    )
    return jax.shard_map(
        on_device, mesh=mesh, in_specs=placed, out_specs=P(("dp", "fsdp"), None), check_vma=False
    )
```

profile of v0, /device:TPU:1, one launch (start us, length us, event | category | flops | bytes accessed | tf_op | source)
XLA Modules:
  0.0 658.2 jit_solution(8967258331673198613)
XLA Ops:
  6.5 0.0 all-gather.3.cloned.1.call-start
  6.6 2.0 pad_maximum_fusion.1
  8.6 0.0 all-gather.3.cloned.1.call-update
  8.6 0.0 all-gather.5.cloned.1.call-start
  8.6 2.0 pad_maximum_fusion
  10.6 0.0 all-gather.5.cloned.1.call-update
  10.7 0.3 fusion.13
  11.0 0.0 copy-start.4
  11.0 1.5 broadcast_in_dim.6
  12.5 7.4 %all-to-all-start = ((f32[8,512,128]{2,1,0:T(8,128)}), f32[8,512,128]{2,1,0:T(8,128)S(1)}, u32[]{:S(2)}, u32[]{:S(2)}) async-start(f32[8,512,128]{2,1,0:T(8,128)} %broadcast_in_dim.6), calls=%async_computation | async-start | bytes 4194304 | tf_op jit(solution)/shard_map/all_to_all | solution.py:18
  19.9 0.1 pad_add_fusion
  19.9 0.1 fusion.20
  20.0 77.4 %all-to-all-done = f32[8,512,128]{2,1,0:T(8,128)S(1)} async-done(((f32[8,512,128]{2,1,0:T(8,128)}), f32[8,512,128]{2,1,0:T(8,128)S(1)}, u32[]{:S(2)}, u32[]{:S(2)}) %all-to-all-start) | async-done | bytes 2097184 | tf_op jit(solution)/shard_map/all_to_all | solution.py:18
  97.4 0.1 reduce_sum.27
  97.5 9.1 %all-gather.3.cloned.1.call-done = bf16[512,4096]{1,0:T(8,128)(2,1)} async-done(((bf16[512,512]{1,0:T(8,128)(2,1)}), bf16[512,4096]{1,0:T(8,128)(2,1)}) %all-gather.3.cloned.1.call-update) | async-done | bytes 4194320 | tf_op jit(solution)/shard_map/all_gather | solution.py:12
  106.6 453.0 %all-gather.5.cloned.1.call-done = bf16[4096,2752]{0,1:T(8,128)(2,1)} async-done(((bf16[128,2752]{0,1:T(8,128)(2,1)}), bf16[4096,2752]{0,1:T(8,128)(2,1)}) %all-gather.5.cloned.1.call-update) | async-done | bytes 22544400 | tf_op jit(solution)/shard_map/all_gather | solution.py:12
  559.7 11.2 %fusion.2 = f32[512,1376]{0,1:T(8,128)} fusion(bf16[512,4096]{1,0:T(8,128)(2,1)} %all-gather.3.cloned.1.call-done, bf16[4096,2752]{0,1:T(8,128)(2,1)} %all-gather.5.cloned.1.call-done), kind=kOutput, calls=%fused_computation.2 | convolution fusion | flops 5771362304 | bytes 18284544 | tf_op jit(solution)/shard_map/dot_general | solution.py:70
  570.9 12.9 %fusion.11 = f32[512,64]{0,1:T(8,128)S(1)} fusion(bf16[1376,64]{0,1:T(8,128)(2,1)S(1)} %copy-done, bf16[512,4096]{1,0:T(8,128)(2,1)} %all-gather.3.cloned.1.call-done, bf16[4096,2752]{0,1:T(8,128)(2,1)} %all-gather.5.cloned.1.call-done, f32[512,1376]{0,1:T(8,128)} %fusion.2), kind=kOutput, calls=%fused_computation.6 | convolution fusion | flops 5865766912 | bytes 18591744 | tf_op jit(solution)/shard_map/dot_general | solution.py:73
  583.8 0.1 reshape.40
  583.9 0.4 convolution_bitcast_fusion
  584.3 13.1 %all_to_all.20 = f32[8,8,8,128]{3,2,1,0:T(8,128)S(1)} all-to-all(f32[8,8,8,128]{3,2,1,0:T(8,128)S(1)} %bitcast.24), channel_id=1, replica_groups=mesh['dp'=8,'tensor'=8,'fsdp'=4] {'tensor'}, dimensions={0} | all-to-all | bytes 524288 | tf_op jit(solution)/shard_map/all_to_all | solution.py:33
  597.5 0.7 broadcast_in_dim.14
  598.2 4.4 all-to-all-start.2
  602.6 8.7 %all-to-all-done.2 = f32[8,8,8,128]{3,2,1,0:T(8,128)S(1)} async-done(((f32[8,8,8,128]{3,2,1,0:T(8,128)}), f32[8,8,8,128]{3,2,1,0:T(8,128)S(1)}, u32[]{:S(2)}, u32[]{:S(2)}) %all-to-all-start.2) | async-done | bytes 262176 | tf_op jit(solution)/shard_map/all_to_all | solution.py:18
  611.3 0.2 multiply_reduce_fusion
  611.4 0.2 bitcast_multiply_fusion
  611.7 0.1 broadcast_in_dim.15
  611.8 22.4 %all_to_all.21 = f32[32,4,1024]{2,1,0:T(4,128)S(1)} all-to-all(f32[32,4,1024]{2,1,0:T(4,128)S(1)} %broadcast_in_dim.15), channel_id=1, replica_groups=mesh['dp'=8,'tensor'=8,'fsdp'=4] {'dp','fsdp'}, dimensions={0} | all-to-all | bytes 1048576 | tf_op jit(solution)/shard_map/all_to_all | solution.py:18
  634.2 0.2 reshape.43
  634.3 0.5 fusion.18
  634.9 15.9 %psum.7 = f32[4,128]{1,0:T(4,128)S(1)} all-reduce(f32[4,128]{1,0:T(4,128)S(1)} %fusion.18), channel_id=1, replica_groups=mesh['dp'=8,'tensor'=8,'fsdp'=4] {'tensor'}, use_global_device_ids=true, to_apply=%region_3.4 | all-reduce | flops 512 | bytes 4096 | tf_op jit(solution)/shard_map/psum | solution.py:100
  650.8 0.6 broadcast_multiply_fusion
  (17 shorter events, 0.1 us)
Async XLA Ops:
  6.5 564.3 %copy-start = (bf16[1376,64]{0,1:T(8,128)(2,1)S(1)}, bf16[1376,64]{0,1:T(8,128)(2,1)}, u32[]{:S(2)}) copy-start(bf16[1376,64]{0,1:T(8,128)(2,1)} %param.18) | copy-start | bytes 528388
  6.5 4.1 copy-start.2
  6.5 4.1 copy-start.1
  6.5 4.1 copy-start.3
  6.5 100.1 %all-gather.3.cloned.1.call-start = ((), (), s32[]{:S(2)}) async-start(), calls=%async_computation.4 | async-start | bytes 4718592 | tf_op jit(solution)/shard_map/all_gather | solution.py:12
  8.6 551.1 %all-gather.5.cloned.1.call-start = ((), (), s32[]{:S(2)}) async-start(), calls=%async_computation.5 | async-start | bytes 23248896 | tf_op jit(solution)/shard_map/all_gather | solution.py:12
  11.0 8.9 %copy-start.4 = (s32[4]{0:T(128)S(1)}, s32[4]{0:T(128)}, u32[]{:S(2)}) copy-start(s32[4]{0:T(128)} %param.15) | copy-start | bytes 52
  11.0 8.9 %copy-start.5 = (s32[4]{0:T(128)S(1)}, s32[4]{0:T(128)}, u32[]{:S(2)}) copy-start(s32[4]{0:T(128)} %param.14) | copy-start | bytes 52
  12.5 84.9 %all-to-all-start = ((f32[8,512,128]{2,1,0:T(8,128)}), f32[8,512,128]{2,1,0:T(8,128)S(1)}, u32[]{:S(2)}, u32[]{:S(2)}) async-start(f32[8,512,128]{2,1,0:T(8,128)} %broadcast_in_dim.6), calls=%async_computation | async-start | bytes 4194304 | tf_op jit(solution)/shard_map/all_to_all | solution.py:18
  598.2 13.1 %all-to-all-start.2 = ((f32[8,8,8,128]{3,2,1,0:T(8,128)}), f32[8,8,8,128]{3,2,1,0:T(8,128)S(1)}, u32[]{:S(2)}, u32[]{:S(2)}) async-start(f32[8,8,8,128]{3,2,1,0:T(8,128)} %broadcast_in_dim.14), calls=%async_computation.2 | async-start | bytes 524288 | tf_op jit(solution)/shard_map/all_to_all | solution.py:18
Sparse Core Ops, SparseCore 0:
  9.1 97.4 all-gather.2
  109.8 449.7 all-gather.4
where the time goes:
time: 659 us; the launch traced here: 658 us
  waiting for transfers between devices  548 us (83%)
  blocking collectives  51.4 us (8%)
  matrix products  25.3 us (4%)
  between operations  13.5 us (2%)
  starting transfers between devices  11.8 us (2%)
    all_gather x2, waiting for transfers between devices, side_by_side(): out = lax.all_gather(both, axis, axis=dim, tiled=True)  462 us
    all_to_all x2, waiting for transfers between devices, from_everyone(): return lax.all_to_all(copies, axis, split_axis=0, concat_axis=0, tiled=True)  86.1 us
    all_to_all x1, blocking collectives, from_everyone(): return lax.all_to_all(copies, axis, split_axis=0, concat_axis=0, tiled=True)  22.4 us
    psum x1, blocking collectives, on_device(): product = lax.psum(partial_scores, 'tensor')  15.9 us
  transfers between devices with their start and end apart: 4, of which 4 were waited for; matrix products, arithmetic and copies ran while one was open for 1% of the time, Pallas kernels for 0%

commit v1 on v0

--- a/solution.py
+++ b/solution.py
@@ -97,7 +97,7 @@
         precision=lax.Precision.HIGHEST,
         preferred_element_type=jnp.float32,
     )
-    product = lax.psum(partial_scores, "tensor")
+    product = jnp.sum(lax.all_gather(partial_scores, "tensor"), 0)
     return product * jnp.sqrt(jnp.float32(width_all))
 
 

time: 659 us -> 658 us (level)
    psum x1 -> x0, blocking collectives: 15.9 us -> none  [on_device(): product = lax.psum(partial_scores, 'tensor')]
    all_gather x0 -> x1, blocking collectives: none -> 15.5 us  [on_device(): product = jnp.sum(lax.all_gather(partial_scores, 'tensor'), 0)]
where the time goes in v1:
time: 658 us
  waiting for transfers between devices  548 us (83%)
  blocking collectives  51 us (8%)
  matrix products  25.3 us (4%)
  between operations  13.5 us (2%)
  starting transfers between devices  11.8 us (2%)
    all_gather x2, waiting for transfers between devices, side_by_side(): out = lax.all_gather(both, axis, axis=dim, tiled=True)  462 us
    all_to_all x2, waiting for transfers between devices, from_everyone(): return lax.all_to_all(copies, axis, split_axis=0, concat_axis=0, tiled=True)  86.1 us
    all_to_all x1, blocking collectives, from_everyone(): return lax.all_to_all(copies, axis, split_axis=0, concat_axis=0, tiled=True)  22.4 us
    all_gather x1, blocking collectives, on_device(): product = jnp.sum(lax.all_gather(partial_scores, 'tensor'), 0)  15.5 us
  transfers between devices with their start and end apart: 4, of which 4 were waited for; matrix products, arithmetic and copies ran while one was open for 1% of the time, Pallas kernels for 0%

profile of v1, /device:TPU:1, one launch (start us, length us, event | category | flops | bytes accessed | tf_op | source)
XLA Modules:
  0.0 657.8 jit_solution(813282748647787219)
XLA Ops:
  6.5 0.0 all-gather.5.cloned.1.call-start
  6.6 2.0 pad_maximum_fusion.1
  8.6 0.0 all-gather.5.cloned.1.call-update
  8.6 0.0 all-gather.7.cloned.1.call-start
  8.6 2.0 pad_maximum_fusion
  10.6 0.0 all-gather.7.cloned.1.call-update
  10.7 0.3 fusion.13
  11.0 0.0 copy-start.4
  11.0 1.5 broadcast_in_dim.6
  12.5 7.4 %all-to-all-start = ((f32[8,512,128]{2,1,0:T(8,128)}), f32[8,512,128]{2,1,0:T(8,128)S(1)}, u32[]{:S(2)}, u32[]{:S(2)}) async-start(f32[8,512,128]{2,1,0:T(8,128)} %broadcast_in_dim.6), calls=%async_computation | async-start | bytes 4194304 | tf_op jit(solution)/shard_map/all_to_all | solution.py:18
  19.9 0.1 pad_add_fusion
  19.9 0.1 fusion.19
  20.0 77.4 %all-to-all-done = f32[8,512,128]{2,1,0:T(8,128)S(1)} async-done(((f32[8,512,128]{2,1,0:T(8,128)}), f32[8,512,128]{2,1,0:T(8,128)S(1)}, u32[]{:S(2)}, u32[]{:S(2)}) %all-to-all-start) | async-done | bytes 2097184 | tf_op jit(solution)/shard_map/all_to_all | solution.py:18
  97.4 0.1 reduce_sum.36
  97.5 9.1 %all-gather.5.cloned.1.call-done = bf16[512,4096]{1,0:T(8,128)(2,1)} async-done(((bf16[512,512]{1,0:T(8,128)(2,1)}), bf16[512,4096]{1,0:T(8,128)(2,1)}) %all-gather.5.cloned.1.call-update) | async-done | bytes 4194320 | tf_op jit(solution)/shard_map/all_gather | solution.py:12
  106.6 453.0 %all-gather.7.cloned.1.call-done = bf16[4096,2752]{0,1:T(8,128)(2,1)} async-done(((bf16[128,2752]{0,1:T(8,128)(2,1)}), bf16[4096,2752]{0,1:T(8,128)(2,1)}) %all-gather.7.cloned.1.call-update) | async-done | bytes 22544400 | tf_op jit(solution)/shard_map/all_gather | solution.py:12
  559.7 11.2 %fusion.2 = f32[512,1376]{0,1:T(8,128)} fusion(bf16[512,4096]{1,0:T(8,128)(2,1)} %all-gather.5.cloned.1.call-done, bf16[4096,2752]{0,1:T(8,128)(2,1)} %all-gather.7.cloned.1.call-done), kind=kOutput, calls=%fused_computation.2 | convolution fusion | flops 5771362304 | bytes 18284544 | tf_op jit(solution)/shard_map/dot_general | solution.py:70
  570.9 12.9 %fusion.11 = f32[512,64]{0,1:T(8,128)S(1)} fusion(bf16[1376,64]{0,1:T(8,128)(2,1)S(1)} %copy-done, bf16[512,4096]{1,0:T(8,128)(2,1)} %all-gather.5.cloned.1.call-done, bf16[4096,2752]{0,1:T(8,128)(2,1)} %all-gather.7.cloned.1.call-done, f32[512,1376]{0,1:T(8,128)} %fusion.2), kind=kOutput, calls=%fused_computation.6 | convolution fusion | flops 5865766912 | bytes 18591744 | tf_op jit(solution)/shard_map/dot_general | solution.py:73
  583.8 0.1 reshape.40
  583.9 0.4 convolution_bitcast_fusion
  584.3 13.1 %all_to_all.20 = f32[8,8,8,128]{3,2,1,0:T(8,128)S(1)} all-to-all(f32[8,8,8,128]{3,2,1,0:T(8,128)S(1)} %bitcast.26), channel_id=1, replica_groups=mesh['dp'=8,'tensor'=8,'fsdp'=4] {'tensor'}, dimensions={0} | all-to-all | bytes 524288 | tf_op jit(solution)/shard_map/all_to_all | solution.py:33
  597.5 0.7 broadcast_in_dim.14
  598.2 4.4 all-to-all-start.2
  602.6 8.7 %all-to-all-done.2 = f32[8,8,8,128]{3,2,1,0:T(8,128)S(1)} async-done(((f32[8,8,8,128]{3,2,1,0:T(8,128)}), f32[8,8,8,128]{3,2,1,0:T(8,128)S(1)}, u32[]{:S(2)}, u32[]{:S(2)}) %all-to-all-start.2) | async-done | bytes 262176 | tf_op jit(solution)/shard_map/all_to_all | solution.py:18
  611.3 0.2 multiply_reduce_fusion
  611.4 0.2 bitcast_multiply_fusion
  611.7 0.1 broadcast_in_dim.15
  611.8 22.4 %all_to_all.21 = f32[32,4,1024]{2,1,0:T(4,128)S(1)} all-to-all(f32[32,4,1024]{2,1,0:T(4,128)S(1)} %broadcast_in_dim.15), channel_id=1, replica_groups=mesh['dp'=8,'tensor'=8,'fsdp'=4] {'dp','fsdp'}, dimensions={0} | all-to-all | bytes 1048576 | tf_op jit(solution)/shard_map/all_to_all | solution.py:18
  634.2 0.2 reshape.43
  634.3 0.5 convolution_bitcast_fusion.1
  634.9 15.5 %all-gather.1 = f32[8,4,128]{2,1,0:T(4,128)S(1)} all-gather(f32[1,4,128]{2,1,0:T(4,128)S(1)} %convolution_bitcast_fusion.1), channel_id=2, replica_groups=mesh['dp'=8,'tensor'=8,'fsdp'=4] {'tensor'}, dimensions={0}, use_global_device_ids=true | all-gather | bytes 18432 | tf_op jit(solution)/shard_map/all_gather | solution.py:100
  650.4 0.6 broadcast_multiply_fusion
  (18 shorter events, 0.2 us)
Async XLA Ops:
  6.5 564.3 %copy-start = (bf16[1376,64]{0,1:T(8,128)(2,1)S(1)}, bf16[1376,64]{0,1:T(8,128)(2,1)}, u32[]{:S(2)}) copy-start(bf16[1376,64]{0,1:T(8,128)(2,1)} %param.18) | copy-start | bytes 528388
  6.5 4.1 copy-start.2
  6.5 4.1 copy-start.1
  6.5 4.1 copy-start.3
  6.5 100.1 %all-gather.5.cloned.1.call-start = ((), (), s32[]{:S(2)}) async-start(), calls=%async_computation.4 | async-start | bytes 4718592 | tf_op jit(solution)/shard_map/all_gather | solution.py:12
  8.6 551.1 %all-gather.7.cloned.1.call-start = ((), (), s32[]{:S(2)}) async-start(), calls=%async_computation.5 | async-start | bytes 23248896 | tf_op jit(solution)/shard_map/all_gather | solution.py:12
  11.0 8.9 %copy-start.4 = (s32[4]{0:T(128)S(1)}, s32[4]{0:T(128)}, u32[]{:S(2)}) copy-start(s32[4]{0:T(128)} %param.15) | copy-start | bytes 52
  11.0 8.9 %copy-start.5 = (s32[4]{0:T(128)S(1)}, s32[4]{0:T(128)}, u32[]{:S(2)}) copy-start(s32[4]{0:T(128)} %param.14) | copy-start | bytes 52
  12.5 84.9 %all-to-all-start = ((f32[8,512,128]{2,1,0:T(8,128)}), f32[8,512,128]{2,1,0:T(8,128)S(1)}, u32[]{:S(2)}, u32[]{:S(2)}) async-start(f32[8,512,128]{2,1,0:T(8,128)} %broadcast_in_dim.6), calls=%async_computation | async-start | bytes 4194304 | tf_op jit(solution)/shard_map/all_to_all | solution.py:18
  598.2 13.1 %all-to-all-start.2 = ((f32[8,8,8,128]{3,2,1,0:T(8,128)}), f32[8,8,8,128]{3,2,1,0:T(8,128)S(1)}, u32[]{:S(2)}, u32[]{:S(2)}) async-start(f32[8,8,8,128]{3,2,1,0:T(8,128)} %broadcast_in_dim.14), calls=%async_computation.2 | async-start | bytes 524288 | tf_op jit(solution)/shard_map/all_to_all | solution.py:18
Sparse Core Ops, SparseCore 0:
  9.1 97.4 all-gather.4
  109.8 449.7 all-gather.6
